TPU v7x, 32 devices: a whole 2x2x4 slice. The times are simulated.
32 devices in a mesh: rows: 8 (over z, y), cols: 4 (over x, core).
Axes of the slice: x: 2, y: 2, z: 4, core: 2. Of those that a mesh axis runs over, the one named last changes fastest.
Arguments:
- weight_up: bfloat16 [12288, 49152], P('rows', 'cols'), may hold values from -0.078125 to 0.078125
- low_up: bfloat16 [12288, 64], P('rows'), may hold values from -0.0546875 to 0.0546875
- high_up: bfloat16 [64, 49152], P(None, 'cols'), may hold values from -0.75 to 0.75
- norm_train: float32 [12288], P(('rows', 'cols')), may hold values from 0.25 to 1.75
- norm_step: float32 [12288], P(('rows', 'cols')), may hold values from -0.3 to 0.3
Outputs:
- serve_up: bfloat16 [12288, 49152], P(None, ('cols', 'rows'))
- scale_up: float32 [49152], P(('cols', 'rows'))
- serve_norm: bfloat16 [12288], replicated
All inputs are finite; a program needn't handle non-finite values.
Results may differ from a plain program's by a relative error of at most 0.0004.
Values may be sent and summed in bfloat16 or wider, within the bound.
A program may use at most 256 MiB of HBM per device.

v0:
```python
import jax
import jax.numpy as jnp
from jax import lax
from jax.sharding import PartitionSpec as P

mix_rate = 0.5


def per_device(weight_up, low_up, high_up, norm_train, norm_step):
    fresh_up = weight_up.astype(jnp.float32) + mix_rate * jnp.dot(
        low_up, high_up, preferred_element_type=jnp.float32
    )
    total_up = lax.psum(jnp.sum(fresh_up * fresh_up, axis=0), "rows")
    scale_up = jnp.sqrt(total_up)
    narrow_up = (fresh_up / scale_up).astype(jnp.bfloat16)
    serve_up = lax.all_to_all(narrow_up, "rows", split_axis=1, concat_axis=0, tiled=True)
    place = lax.axis_index("rows")
    scale_up = lax.dynamic_slice_in_dim(scale_up, place * serve_up.shape[1], serve_up.shape[1])
    serve_norm = lax.all_gather(
        (norm_train + norm_step).astype(jnp.bfloat16), ("rows", "cols"), axis=0, tiled=True
    )
    return (serve_up, scale_up, serve_norm)


def solution(mesh):
    in_specs = (
        P("rows", "cols"),
        P("rows", None),
        P(None, "cols"),
        P(("rows", "cols")),
        P(("rows", "cols")),
    )
    out_specs = (P(None, ("cols", "rows")), P(("cols", "rows")), P())
    return jax.shard_map(
        per_device, mesh=mesh, in_specs=in_specs, out_specs=out_specs, check_vma=False
    )
```

profile of v0, /device:TPU:17, one launch (start us, length us, event | category | flops | bytes accessed | tf_op | source)
XLA Modules:
  0.0 1004.8 jit_solution(14810098583701876798)
XLA Ops:
  0.6 0.0 copy-start
  0.6 1.4 copy-done
  2.0 38.1 %multiply_reduce_fusion = (f32[12288]{0:T(1024)S(1)}, f32[1536,12288]{1,0:T(8,128)}) fusion(bf16[1536,64]{0,1:T(8,128)(2,1)} %param.6, bf16[64,12288]{1,0:T(8,128)(2,1)S(1)} %copy-done, bf16[1536,12288]{1,0:T(8,128)(2,1)} %param.5), kind=kOutput, calls=%fused_computation.1 | convolution fusion | flops 2510278656 | bytes 115064832 | tf_op jit(solution)/shard_map/dot_general | solution.py:10
  40.1 25.9 %psum.7 = f32[12288]{0:T(1024)S(1)} all-reduce(f32[12288]{0:T(1024)S(1)} %get-tuple-element.3), channel_id=1, replica_groups=mesh['rows'=8,'cols'=4] {'rows'}, use_global_device_ids=true, to_apply=%region_1.0 | all-reduce | flops 12288 | bytes 98304 | tf_op jit(solution)/shard_map/psum | solution.py:13
  66.0 36.5 %divide_convert_fusion = bf16[1536,12288]{1,0:T(8,128)(2,1)} fusion(f32[1536,12288]{1,0:T(8,128)} %get-tuple-element.4, f32[12288]{0:T(1024)S(1)} %sqrt.3), kind=kLoop, calls=%fused_computation | loop fusion | flops 37748736 | bytes 113295360 | tf_op jit(solution)/shard_map/convert_element_type | solution.py:15
  102.5 26.0 %copy.13 = bf16[192,8,8,1536]{3,2,0,1:T(8,128)(2,1)} copy(bf16[192,8,8,1536]{3,2,1,0:T(8,128)(2,1)} %bitcast.10) | data formatting | bytes 75497472 | tf_op jit(solution)/shard_map/all_to_all | solution.py:16
  128.5 0.0 copy-start.2
  128.5 0.0 copy-start.3
  128.5 12.3 %all-to-all-start = ((bf16[1536,8,1536]{2,0,1:T(8,128)(2,1)}), bf16[1536,8,1536]{2,0,1:T(8,128)(2,1)}, u32[]{:S(2)}, u32[]{:S(2)}) async-start(bf16[1536,8,1536]{2,0,1:T(8,128)(2,1)} %bitcast.9), calls=%async_computation | async-start | bytes 75497472 | tf_op jit(solution)/shard_map/all_to_all | solution.py:16
  140.8 0.7 dynamic_slice.3
  141.5 0.0 copy-done.2
  141.5 0.0 copy-done.3
  141.5 836.8 %all-gather = bf16[32,1,384]{2,1,0:T(2,128)(2,1)S(1)} all-gather(bf16[1,1,384]{2,1,0:T(2,128)(2,1)S(1)} %reshape.10), channel_id=1, replica_groups=mesh['rows'=8,'cols'=4] {'rows','cols'}, dimensions={0}, use_global_device_ids=true | all-gather | bytes 25344 | tf_op jit(solution)/shard_map/all_gather | solution.py:19
  978.3 0.1 reduce
  978.5 0.6 reshape.11
  979.1 0.0 all-to-all-done
  979.1 0.0 copy-start.1
  979.1 25.7 %copy.15 = bf16[12288,1536]{1,0:T(8,128)(2,1)} copy(bf16[12288,1536]{1,0:T(8,128)(2,1)} %bitcast.1) | data formatting | bytes 75497472
  1004.8 0.0 copy-done.1
  (3 shorter events, 0.0 us)
Async XLA Ops:
  0.6 1.4 copy-start
  128.5 13.0 %copy-start.2 = (f32[384]{0:T(512)S(1)}, f32[384]{0:T(512)}, u32[]{:S(2)}) copy-start(f32[384]{0:T(512)} %param.8) | copy-start | bytes 4612
  128.5 13.0 %copy-start.3 = (f32[384]{0:T(512)S(1)}, f32[384]{0:T(512)}, u32[]{:S(2)}) copy-start(f32[384]{0:T(512)} %param.9) | copy-start | bytes 4612
  128.5 850.6 %all-to-all-start = ((bf16[1536,8,1536]{2,0,1:T(8,128)(2,1)}), bf16[1536,8,1536]{2,0,1:T(8,128)(2,1)}, u32[]{:S(2)}, u32[]{:S(2)}) async-start(bf16[1536,8,1536]{2,0,1:T(8,128)(2,1)} %bitcast.9), calls=%async_computation | async-start | bytes 75497472 | tf_op jit(solution)/shard_map/all_to_all | solution.py:16
  979.1 25.8 %copy-start.1 = (bf16[64,12288]{1,0:T(8,128)(2,1)S(1)}, bf16[64,12288]{1,0:T(8,128)(2,1)}, u32[]{:S(2)}) copy-start(bf16[64,12288]{1,0:T(8,128)(2,1)} %param.7) | copy-start | bytes 4718596
where the time goes:
time: 1010 us; the launch traced here: 1000 us
  blocking collectives  863 us (85%)
  local copies, waits for them, and re-layouts  54.5 us (5%)
  matrix products  38.1 us (4%)
  other arithmetic  36.6 us (4%)
  starting transfers between devices  12.3 us (1%)
    all_gather x1, blocking collectives, per_device(): lax.all_gather((norm_train + norm_step).astype(jnp.bfloat16), ('rows', 'c...  837 us
    dot_general x1, matrix products, per_device(): jnp.dot(low_up, high_up, preferred_element_type=jnp.float32)  38.1 us
    convert_element_type x1, other arithmetic, per_device(): narrow_up = (fresh_up / scale_up).astype(jnp.bfloat16)  36.5 us
    unnamed x11, local copies, waits for them, and re-layouts  27.8 us
    all_to_all x1, local copies, waits for them, and re-layouts, per_device(): lax.all_to_all(narrow_up, 'rows', split_axis=1, concat_axis=0, tiled=True)  26 us
    psum x1, blocking collectives, per_device(): total_up = lax.psum(jnp.sum(fresh_up * fresh_up, axis=0), 'rows')  25.9 us
  transfers between devices with their start and end apart: 1, of which 0 were waited for; matrix products, arithmetic and copies ran while one was open for 0% of the time, Pallas kernels for 0%

commit v1 on v0

--- a/solution.py
+++ b/solution.py
@@ -1,12 +1,258 @@
+import functools
+
 import jax
 import jax.numpy as jnp
 from jax import lax
+from jax.experimental import pallas as pl
+from jax.experimental.pallas import tpu as pltpu
 from jax.sharding import PartitionSpec as P
 
 mix_rate = 0.5
-
-
-def per_device(weight_up, low_up, high_up, norm_train, norm_step):
+MESH = pl.DeviceIdType.MESH
+LANES = 128
+AHEAD = 4
+
+
+def partner(me, step, ranks):
+    if ranks & (ranks - 1):
+        return lax.rem(me + step, ranks)
+    bit, other = 1, me
+    while bit < ranks:
+        if step & bit:
+            other = other + bit - 2 * bit * lax.rem(other // bit, 2)
+        bit *= 2
+    return other
+
+
+def source(me, step, ranks):
+    if ranks & (ranks - 1):
+        return lax.rem(me + ranks - step, ranks)
+    return partner(me, step, ranks)
+
+
+def kernel(
+    ranks, teams, w_ref, low_ref, high_ref, norm_ref, serve_ref, scale_ref, norm_out,
+    held, fresh, low_all, norm_all, high_own, high_two,
+    send_sem, recv_sem, own_sem, out_sem, high_sem,
+    low_send, low_recv, low_own, norm_send, norm_recv, norm_own,
+    low_send2, low_recv2, norm_send2, norm_recv2,
+):
+    me, team = lax.axis_index("rows"), lax.axis_index("cols")
+    rows, columns = w_ref.shape
+    share = columns // ranks
+    pieces = share // LANES
+    part = low_ref.shape[0] // teams
+    rank = high_ref.shape[0]
+    steps = list(range(ranks - 1, 0, -1))
+
+    def window(owner, piece):
+        return pl.ds(pl.multiple_of(owner * share + piece * LANES, LANES), LANES)
+
+    def block(owner):
+        return pl.ds(pl.multiple_of(owner * rows, 16), rows)
+
+    def piece_copy(piece, to, source_rank):
+        return pltpu.make_async_remote_copy(
+            src_ref=w_ref.at[:, window(to, piece)],
+            dst_ref=held.at[piece, block(me)],
+            send_sem=send_sem.at[piece, to],
+            recv_sem=recv_sem.at[piece, source_rank],
+            device_id={"rows": to},
+            device_id_type=MESH,
+        )
+
+    def piece_own(piece):
+        return pltpu.make_async_copy(
+            w_ref.at[:, window(me, piece)], held.at[piece, block(me)], own_sem.at[piece]
+        )
+
+    def issue(piece):
+        for step in steps:
+            piece_copy(piece, partner(me, step, ranks), me).start()
+        piece_own(piece).start()
+
+    def low_copy(to, source_rank):
+        return pltpu.make_async_remote_copy(
+            src_ref=low_ref.at[pl.ds(pl.multiple_of(team * part, 16), part)],
+            dst_ref=low_all.at[team, me],
+            send_sem=low_send.at[to],
+            recv_sem=low_recv.at[source_rank],
+            device_id={"rows": to},
+            device_id_type=MESH,
+        )
+
+    def norm_copy(to, source_rank):
+        return pltpu.make_async_remote_copy(
+            src_ref=norm_ref,
+            dst_ref=norm_all.at[team, me],
+            send_sem=norm_send.at[to],
+            recv_sem=norm_recv.at[source_rank],
+            device_id={"rows": to},
+            device_id_type=MESH,
+        )
+
+    def team_copy(buffer, sends, receives, to, source_team):
+        return pltpu.make_async_remote_copy(
+            src_ref=buffer.at[team],
+            dst_ref=buffer.at[team],
+            send_sem=sends.at[to],
+            recv_sem=receives.at[source_team],
+            device_id={"cols": to},
+            device_id_type=MESH,
+        )
+
+    high_copy = pltpu.make_async_copy(
+        high_ref.at[:, pl.ds(pl.multiple_of(me * share, LANES), share)], high_own, high_sem
+    )
+    high_copy.start()
+
+    barrier = pltpu.get_barrier_semaphore()
+    for step in steps:
+        pl.semaphore_signal(
+            barrier, inc=1, device_id={"rows": partner(me, step, ranks)}, device_id_type=MESH
+        )
+    for step in range(1, teams):
+        pl.semaphore_signal(
+            barrier, inc=1, device_id={"cols": lax.rem(team + step, teams)}, device_id_type=MESH
+        )
+    pl.semaphore_wait(barrier, ranks - 1 + teams - 1)
+
+    for step in steps:
+        low_copy(partner(me, step, ranks), me).start()
+        norm_copy(partner(me, step, ranks), me).start()
+    low_mine = pltpu.make_async_copy(
+        low_ref.at[pl.ds(pl.multiple_of(team * part, 16), part)], low_all.at[team, me], low_own
+    )
+    norm_mine = pltpu.make_async_copy(norm_ref, norm_all.at[team, me], norm_own)
+    low_mine.start()
+    norm_mine.start()
+
+    ahead = min(AHEAD, pieces)
+
+    @pl.loop(0, ahead)
+    def _(piece):
+        issue(piece)
+
+    high_copy.wait()
+    high_two[...] = jnp.zeros_like(high_two)
+    for piece in range(pieces):
+        now = high_own[:, piece * LANES:(piece + 1) * LANES]
+        high_two[piece, 0:rank, 0:LANES] = now
+        high_two[piece, rank:2 * rank, LANES:2 * LANES] = now
+
+    low_mine.wait()
+    norm_mine.wait()
+    for step in steps:
+        low_copy(partner(me, step, ranks), source(me, step, ranks)).wait()
+        norm_copy(partner(me, step, ranks), source(me, step, ranks)).wait()
+    for step in range(1, teams):
+        to = lax.rem(team + step, teams)
+        team_copy(low_all, low_send2, low_recv2, to, team).start()
+        team_copy(norm_all, norm_send2, norm_recv2, to, team).start()
+    for step in range(1, teams):
+        to, back = lax.rem(team + step, teams), lax.rem(team + teams - step, teams)
+        team_copy(low_all, low_send2, low_recv2, to, back).wait()
+        team_copy(norm_all, norm_send2, norm_recv2, to, back).wait()
+    norm_out[...] = norm_all[...]
+
+    def gather_block(piece, owner, total):
+        def one(quarter, total):
+            both = mix_rate * jnp.dot(
+                low_all[quarter, owner], high_two[piece], preferred_element_type=jnp.float32
+            )
+            for half in range(2):
+                at = pl.multiple_of(owner * rows + half * (rows // 2) + quarter * part, 16)
+                now = held[piece, pl.ds(at, part), :].astype(jnp.float32)
+                now = now + both[:, half * LANES:(half + 1) * LANES]
+                fresh[pl.ds(at, part), :] = now
+                total = total + jnp.sum((now * now).reshape(part // 8, 8, LANES), axis=0)
+            return total
+        return lax.fori_loop(0, teams, one, total)
+
+    tile = rows // teams
+
+    @pl.loop(0, pieces)
+    def _(piece):
+        piece_own(piece).wait()
+        total = gather_block(piece, me, jnp.zeros((8, LANES), jnp.float32))
+        for step in reversed(steps):
+            back = source(me, step, ranks)
+            piece_copy(piece, partner(me, step, ranks), back).wait_recv()
+            total = gather_block(piece, back, total)
+
+        @pl.when(piece + ahead < pieces)
+        def _():
+            issue(piece + ahead)
+
+        scale = jnp.sqrt(jnp.sum(total, axis=0, keepdims=True))
+        scale_ref[pl.ds(piece, 1), :] = scale
+        inverse = 1.0 / scale
+
+        @pl.loop(0, ranks * teams)
+        def _(index):
+            span = pl.ds(pl.multiple_of(index * tile, 16), tile)
+            held[piece, span, :] = (fresh[span, :] * inverse).astype(jnp.bfloat16)
+
+        pltpu.make_async_copy(
+            held.at[piece],
+            serve_ref.at[:, pl.ds(pl.multiple_of(piece * LANES, LANES), LANES)],
+            out_sem.at[piece],
+        ).start()
+
+    @pl.loop(0, pieces)
+    def _(piece):
+        for step in steps:
+            piece_copy(piece, partner(me, step, ranks), me).wait_send()
+        pltpu.make_async_copy(
+            held.at[piece],
+            serve_ref.at[:, pl.ds(pl.multiple_of(piece * LANES, LANES), LANES)],
+            out_sem.at[piece],
+        ).wait()
+
+
+def with_kernel(ranks, teams, weight_up, low_up, high_up, norm_train, norm_step):
+    rows, columns = weight_up.shape
+    rank = low_up.shape[1]
+    share = columns // ranks
+    pieces = share // LANES
+    part = rows // 2 // teams
+    low_two = jnp.concatenate([low_up[:rows // 2], low_up[rows // 2:]], axis=1)
+    norm = (norm_train + norm_step).reshape(1, -1)
+    width = norm.shape[1]
+    dma = pltpu.SemaphoreType.DMA
+    serve_up, scale_up, norm_all = pl.pallas_call(
+        functools.partial(kernel, ranks, teams),
+        out_shape=(
+            jax.ShapeDtypeStruct((ranks * rows, share), jnp.bfloat16),
+            jax.ShapeDtypeStruct((pieces, LANES), jnp.float32),
+            jax.ShapeDtypeStruct((teams, ranks, 1, width), jnp.float32),
+        ),
+        in_specs=[pl.BlockSpec(memory_space=pl.ANY)] * 4,
+        out_specs=(
+            pl.BlockSpec(memory_space=pl.ANY),
+            pl.BlockSpec(memory_space=pltpu.VMEM),
+            pl.BlockSpec(memory_space=pltpu.VMEM),
+        ),
+        scratch_shapes=[
+            pltpu.VMEM((pieces, ranks * rows, LANES), jnp.bfloat16),
+            pltpu.VMEM((ranks * rows, LANES), jnp.float32),
+            pltpu.VMEM((teams, ranks, part, 2 * rank), jnp.bfloat16),
+            pltpu.VMEM((teams, ranks, 1, width), jnp.float32),
+            pltpu.VMEM((rank, share), jnp.bfloat16),
+            pltpu.VMEM((pieces, 2 * rank, 2 * LANES), jnp.bfloat16),
+            dma((pieces, ranks)), dma((pieces, ranks)), dma((pieces,)), dma((pieces,)), dma,
+            dma((ranks,)), dma((ranks,)), dma, dma((ranks,)), dma((ranks,)), dma,
+            dma((teams,)), dma((teams,)), dma((teams,)), dma((teams,)),
+        ],
+        compiler_params=pltpu.CompilerParams(
+            collective_id=0, has_side_effects=True, vmem_limit_bytes=60 * 1024 * 1024
+        ),
+    )(weight_up, low_two, high_up, norm)
+    serve_norm = norm_all.reshape(teams, ranks, width).transpose(1, 0, 2).reshape(-1)
+    return serve_up, scale_up.reshape(-1), serve_norm.astype(jnp.bfloat16)
+
+
+def with_collectives(weight_up, low_up, high_up, norm_train, norm_step):
     fresh_up = weight_up.astype(jnp.float32) + mix_rate * jnp.dot(
         low_up, high_up, preferred_element_type=jnp.float32
     )
@@ -23,6 +269,17 @@
 
 
 def solution(mesh):
+    ranks, teams = mesh.shape["rows"], mesh.shape["cols"]
+
+    def per_device(weight_up, low_up, high_up, norm_train, norm_step):
+        rows, columns = weight_up.shape
+        share, rank = columns // ranks, low_up.shape[1]
+        aligned = share % LANES == 0 and rows % (32 * teams) == 0 and 2 * rank == LANES
+        fits = 2 * ranks * rows * share < 40 * 1024 * 1024
+        if aligned and fits:
+            return with_kernel(ranks, teams, weight_up, low_up, high_up, norm_train, norm_step)
+        return with_collectives(weight_up, low_up, high_up, norm_train, norm_step)
+
     in_specs = (
         P("rows", "cols"),
         P("rows", None),

time: 1010 us -> 884 us (0.88)
  blocking collectives: 863 us -> 0 us
  Pallas kernels: 0 us -> 840 us
  matrix products: 38.1 us -> 0 us
  other arithmetic: 36.6 us -> 2.35 us
  local copies, waits for them, and re-layouts: 54.5 us -> 29 us
  starting transfers between devices: 12.3 us -> 0 us
    pallas_call x0 -> x1, Pallas kernels: none -> 840 us  [with_kernel(): pl.pallas_call(functools.partial(kernel, ranks, teams), out_shape=(jax.Sh...]
    all_gather x1 -> x0, blocking collectives: 837 us -> none  [per_device(): lax.all_gather((norm_train + norm_step).astype(jnp.bfloat16), ('rows', 'c...]
    dot_general x1 -> x0, matrix products: 38.1 us -> none  [per_device(): jnp.dot(low_up, high_up, preferred_element_type=jnp.float32)]
    convert_element_type x2 -> x1, other arithmetic: 36.5 us -> 0.83 us  [with_kernel(): return (serve_up, scale_up.reshape(-1), serve_norm.astype(jnp.bfloat16))]
    all_to_all x1 -> x0, local copies, waits for them, and re-layouts: 26 us -> none  [per_device(): lax.all_to_all(narrow_up, 'rows', split_axis=1, concat_axis=0, tiled=True)]
    psum x1 -> x0, blocking collectives: 25.9 us -> none  [per_device(): total_up = lax.psum(jnp.sum(fresh_up * fresh_up, axis=0), 'rows')]
    all_to_all x1 -> x0, starting transfers between devices: 12.3 us -> none  [per_device(): lax.all_to_all(narrow_up, 'rows', split_axis=1, concat_axis=0, tiled=True)]
    unnamed x11 -> x7, local copies, waits for them, and re-layouts: 27.8 us -> 26.8 us
  transfers between devices with their start and end apart: 1 -> 0, of which waited for: 0 -> 0; matrix products, arithmetic and copies ran while one was open for 0% -> 0% of each run, Pallas kernels for 0% -> 0%
where the time goes in v1:
time: 884 us; the launch traced here: 872 us
  Pallas kernels  840 us (95%)
  local copies, waits for them, and re-layouts  29 us (3%)
    pallas_call x1, Pallas kernels, with_kernel(): pl.pallas_call(functools.partial(kernel, ranks, teams), out_shape=(jax.Sh...  840 us
    unnamed x7, local copies, waits for them, and re-layouts  26.8 us

profile of v1, /device:TPU:17, one launch (start us, length us, event | category | flops | bytes accessed | tf_op | source)
XLA Modules:
  0.0 872.0 jit_solution(9815148145496617873)
XLA Ops:
  0.6 0.7 add.3
  1.3 0.6 reshape.16.norm_ref
  1.9 1.0 fusion
  2.9 0.2 copy.14
  3.0 0.2 copy.15
  3.2 0.8 pad_maximum_fusion.low_ref
  4.0 840.0 %shard_map.76 = (bf16[12288,1536]{1,0:T(8,128)(2,1)}, f32[12,128]{1,0:T(8,128)}, f32[4,8,1,384]{3,2,1,0:T(1,128)}) custom-call(bf16[1536,12288]{1,0:T(8,128)(2,1)} %w_ref.1, bf16[768,128]{1,0:T(8,128)(2,1)} %pad_maximum_fusion.low_ref, bf16[64,12288]{1,0:T(8,128)(2,1)} %high_ref.1, f32[1,384]{1,0:T(1,128)} %reshape.16.norm_ref), custom_call_target="tpu_custom_call" | custom-call | tf_op jit(solution)/shard_map/pallas_call | solution.py:223
  844.0 0.8 convert_element_type.12
  844.9 0.6 convert_element_type.15
  845.5 0.0 copy-start
  845.5 25.9 %copy.20 = bf16[12288,1536]{1,0:T(8,128)(2,1)} copy(bf16[12288,1536]{1,0:T(8,128)(2,1)} %get-tuple-element.14) | data formatting | bytes 75497472
  871.4 0.0 copy-done
  871.4 0.6 copy.21
  (2 shorter events, 0.0 us)
Async XLA Ops:
  845.5 25.9 %copy-start = (f32[12,128]{1,0:T(8,128)S(1)}, f32[12,128]{1,0:T(8,128)}, u32[]{:S(2)}) copy-start(f32[12,128]{1,0:T(8,128)} %get-tuple-element.7) | copy-start | bytes 18436
